TPU v7x, 256 devices: a whole 4x4x8 slice. The times are simulated.
256 devices in a mesh: batch: 128 (over x_hi, y, z, core), rep: 2 (over x_lo).
Axes of the slice: x: 4 (x_hi: 2, x_lo: 2; x = x_hi * 2 + x_lo), y: 4, z: 8, core: 2. Of those that a mesh axis runs over, the one named last changes fastest.
Arguments:
- image_embed: bfloat16 [16384, 1024], P('batch'), may hold values from -2 to 2
- text_embed: bfloat16 [16384, 1024], P(('batch', 'rep')), may hold values from -2 to 2
- logit_scale: float32 [1], replicated, may hold values from 50 to 100
Outputs:
- mean_loss: float32 [], replicated
- image_grad: float32 [16384, 1024], P(('batch', 'rep'))
- text_grad: float32 [16384, 1024], P(('batch', 'rep'))
All inputs are finite; a program needn't handle non-finite values.
Results may differ from a plain program's by a relative error of at most 0.0025.
Values may be sent and summed in bfloat16 or wider, within the bound.
No kernel may reach another device: no remote copies, remote signals or barrier semaphores. Data moves between devices by JAX's collectives and lax.ppermute only.
A program may use at most 128 MiB of HBM per device.

v0:
```python
import functools
import jax
import jax.numpy as jnp
from jax import lax
from jax.sharding import Mesh
from jax.sharding import PartitionSpec as P

BATCH = ("batch_0", "batch_1", "batch_2", "batch_3")
BATCH_REP = ("batch_0", "batch_1", "batch_2", "batch_3", "rep")


def copy_for_each(array, axis):
    peers = lax.axis_size(axis)
    return lax.all_to_all(
        jnp.broadcast_to(array[None], (peers, *array.shape)), axis, 0, 0, tiled=True
    )


def all_in_one(array, axis):
    leaves = jax.tree.leaves(array)
    sequence = sorted(range(len(leaves)), key=lambda k: -leaves[k].size)
    width = (1, *leaves[sequence[0]].shape)[-1]
    lines = [
        jnp.pad(leaves[k].reshape(-1), (0, -leaves[k].size % width)).reshape(-1, width)
        for k in sequence
    ]
    both, at, found = (copy_for_each(jnp.concatenate(lines), axis), 0, {})
    for k, line in zip(sequence, lines):
        share = both[:, at : at + len(line)].reshape(len(both), -1)
        found[k] = share[:, : leaves[k].size].reshape(-1, *leaves[k].shape)
        at += len(line)
    numbers = iter(range(len(leaves)))
    return jax.tree.map(lambda _: found[next(numbers)], array)


def joined_by_halves(pieces, combine):
    while len(jax.tree.leaves(pieces)[0]) > 1:
        pieces = jax.vmap(combine)(
            *(jax.tree.map(lambda part: part[side::2], pieces) for side in (0, 1))
        )
    return jax.tree.map(lambda part: part[0], pieces)


def merged(array, axis, combine):
    pieces = all_in_one(array, axis)
    return joined_by_halves(pieces, combine)


def collected_together(array, axis):
    leaves = jax.tree.leaves(array)
    sequence = sorted(range(len(leaves)), key=lambda k: -leaves[k].size)
    width = (1, *leaves[sequence[0]].shape)[-1]
    lines = [
        jnp.pad(leaves[k].reshape(-1), (0, -leaves[k].size % width)).reshape(-1, width)
        for k in sequence
    ]
    both, at, found = (lax.all_gather(jnp.concatenate(lines), axis), 0, {})
    for k, line in zip(sequence, lines):
        share = both[:, at : at + len(line)].reshape(len(both), -1)
        found[k] = share[:, : leaves[k].size].reshape(-1, *leaves[k].shape)
        at += len(line)
    numbers = iter(range(len(leaves)))
    return jax.tree.map(lambda _: found[next(numbers)], array)


def merged_by_axis(array, axes, combine):
    for axis in axes:
        pieces = collected_together(array, axis)
        array = jax.tree.map(lambda part: part[0], pieces)
        for k in range(1, lax.axis_size(axis)):
            array = combine(array, jax.tree.map(lambda part: part[k], pieces))
    return array


def over_axes(array, axes):
    return functools.reduce(lax.psum, axes, array)


def cut_along(array, dim, peers):
    lengths = array.shape
    parts = array.reshape(*lengths[:dim], peers, lengths[dim] // peers, *lengths[dim + 1 :])
    return jnp.moveaxis(parts, dim, 0)


def sum_at_owner(array, axis, dim):
    parts = cut_along(array, dim, lax.axis_size(axis))
    arrived = lax.all_to_all(parts, axis, split_axis=0, concat_axis=0, tiled=True)
    return arrived.sum(axis=0)


def combine_lse(earlier, later):
    biggest = jnp.maximum(earlier[0], later[0])
    return (
        biggest,
        earlier[1] * jnp.exp(earlier[0] - biggest) + later[1] * jnp.exp(later[0] - biggest),
    )


def body(image_embed, text_embed, logit_scale):
    scale_value = logit_scale[0]
    row_count = image_embed.shape[0]
    half_rows = text_embed.shape[0]
    batch_count = lax.axis_size(BATCH)
    batch_index = lax.axis_index(BATCH)
    rep_index = lax.axis_index("rep")
    whole_text = lax.all_gather(text_embed, BATCH, axis=0, tiled=True)
    scores = scale_value * lax.dot_general(
        image_embed, whole_text, (((1,), (1,)), ((), ())), preferred_element_type=jnp.float32
    )
    row_max = jnp.max(scores, axis=1)
    row_sum = jnp.sum(jnp.exp(scores - row_max[:, None]), axis=1)
    row_max, row_sum = merged((row_max, row_sum), "rep", combine_lse)
    row_lse = row_max + jnp.log(row_sum)
    column_max = jnp.max(scores, axis=0)
    column_sum = jnp.sum(jnp.exp(scores - column_max[None, :]), axis=0)
    column_max, column_sum = merged_by_axis((column_max, column_sum), BATCH, combine_lse)
    col_lse = column_max + jnp.log(column_sum)
    own_lse = lax.dynamic_slice_in_dim(col_lse, batch_index * half_rows, half_rows, 0)
    own_scores = lax.dynamic_slice(
        scores, (rep_index * half_rows, batch_index * half_rows), (half_rows, half_rows)
    )
    own_diag = jnp.diagonal(own_scores)
    own_rows = lax.dynamic_slice_in_dim(row_lse, rep_index * half_rows, half_rows, 0)
    loss_sum = over_axes(jnp.sum(own_rows + own_lse - 2.0 * own_diag), BATCH_REP)
    mean_loss = loss_sum / (2 * row_count * batch_count)
    row_ids = lax.broadcasted_iota(jnp.int32, scores.shape, 0) - rep_index * half_rows
    column_ids = lax.broadcasted_iota(jnp.int32, scores.shape, 1) - batch_index * half_rows
    diag_match = ((row_ids == column_ids) & (column_ids >= 0) & (column_ids < half_rows)).astype(
        jnp.float32
    )
    weights = (
        jnp.exp(scores - row_lse[:, None]) + jnp.exp(scores - col_lse[None, :]) - 2.0 * diag_match
    ).astype(jnp.bfloat16)
    image_part = (
        scale_value * 0.5 * jnp.dot(weights, whole_text, preferred_element_type=jnp.float32)
    )
    image_grad = sum_at_owner(image_part, "rep", 0)
    all_rows_lse = lax.all_gather(row_lse, BATCH, axis=0, tiled=True)
    own_first = (2 * batch_index + rep_index) * half_rows
    fragment = lax.all_gather(image_embed, BATCH, axis=0, tiled=True)
    scores_back = scale_value * lax.dot_general(
        text_embed, fragment, (((1,), (1,)), ((), ())), preferred_element_type=jnp.float32
    )
    image_ids = lax.broadcasted_iota(jnp.int32, scores_back.shape, 1)
    text_ids = own_first + lax.broadcasted_iota(jnp.int32, scores_back.shape, 0)
    back_match = (image_ids == text_ids).astype(jnp.float32)
    weights_block = (
        jnp.exp(scores_back - own_lse[:, None])
        + jnp.exp(scores_back - all_rows_lse[None, :])
        - 2.0 * back_match
    ).astype(jnp.bfloat16)
    summed = jnp.dot(weights_block, fragment, preferred_element_type=jnp.float32)
    text_grad = scale_value * 0.5 * summed
    return (mean_loss, image_grad, text_grad)


def solution(mesh):
    split = Mesh(
        mesh.devices.reshape(2, 4, 8, 2, mesh.shape["rep"]),
        ("batch_0", "batch_1", "batch_2", "batch_3", "rep"),
    )
    placed = (P(BATCH, None), P(BATCH_REP, None), P())
    return jax.shard_map(
        body,
        mesh=split,
        in_specs=placed,
        out_specs=(P(), P(BATCH_REP, None), P(BATCH_REP, None)),
        check_vma=False,
    )
```

profile of v0, /device:TPU:1, one launch (start us, length us, event | category | flops | bytes accessed | tf_op | source)
XLA Modules:
  0.0 527.8 jit_solution(11438516798877127760)
XLA Ops:
  7.2 0.7 all-gather.12.cloned.1.call-update
  7.9 0.7 all-gather.14.cloned.1.call-update
  9.4 157.7 %all-gather.12.cloned.1.call-done = bf16[8192,1024]{1,0:T(8,128)(2,1)} async-done(((bf16[64,1024]{1,0:T(8,128)(2,1)}), bf16[8192,1024]{1,0:T(8,128)(2,1)}) %all-gather.12.cloned.1.call-update) | async-done | bytes 16777232 | tf_op jit(solution)/shard_map/all_gather | solution.py:106
  167.1 13.5 %fusion.72 = (f32[128]{0:T(128)S(1)}, f32[8192]{0:T(1024)S(1)}, f32[128,8192]{1,0:T(8,128)}) fusion(bf16[128,1024]{1,0:T(8,128)(2,1)} %param.3, bf16[8192,1024]{1,0:T(8,128)(2,1)} %all-gather.12.cloned.1.call-done, f32[]{:T(128)} %bitcast.315), kind=kOutput, calls=%fused_computation.126 | convolution fusion | flops 2150621184 | bytes 21266948 | tf_op jit(solution)/shard_map/dot_general | solution.py:107
  180.7 3.6 exponential_reduce_fusion.1
  184.2 0.6 broadcast_in_dim.4
  184.8 3.2 all-to-all-start
  188.1 0.1 maximum_bitcast_fusion
  188.1 5.3 %all-gather.4 = f32[2,2,8192]{2,1,0:T(2,128)S(1)} all-gather(f32[1,2,8192]{2,1,0:T(2,128)S(1)} %maximum_bitcast_fusion), channel_id=2, replica_groups=mesh['batch_0'=2,'batch_1'=4,'batch_2'=8,'batch_3'=2,'rep'=2] {'batch_0'}, dimensions={0}, use_global_device_ids=true | all-gather | bytes 196608 | tf_op jit(solution)/shard_map/all_gather | solution.py:57
  193.4 0.1 fusion.47
  193.5 0.1 maximum_bitcast_fusion.1
  193.6 11.0 %all-gather.5 = f32[4,2,8192]{2,1,0:T(2,128)S(1)} all-gather(f32[1,2,8192]{2,1,0:T(2,128)S(1)} %maximum_bitcast_fusion.1), channel_id=3, replica_groups=mesh['batch_0'=2,'batch_1'=4,'batch_2'=8,'batch_3'=2,'rep'=2] {'batch_1'}, dimensions={0}, use_global_device_ids=true | all-gather | bytes 327680 | tf_op jit(solution)/shard_map/all_gather | solution.py:57
  204.6 0.3 fusion.38
  204.9 0.1 maximum_bitcast_fusion.2
  205.0 21.2 %all-gather.6 = f32[8,2,8192]{2,1,0:T(2,128)S(1)} all-gather(f32[1,2,8192]{2,1,0:T(2,128)S(1)} %maximum_bitcast_fusion.2), channel_id=4, replica_groups=mesh['batch_0'=2,'batch_1'=4,'batch_2'=8,'batch_3'=2,'rep'=2] {'batch_2'}, dimensions={0}, use_global_device_ids=true | all-gather | bytes 589824 | tf_op jit(solution)/shard_map/all_gather | solution.py:57
  226.2 0.7 fusion.17
  226.9 0.1 maximum_bitcast_fusion.3
  227.0 9.8 %all-gather.7 = f32[2,2,8192]{2,1,0:T(2,128)S(1)} all-gather(f32[1,2,8192]{2,1,0:T(2,128)S(1)} %maximum_bitcast_fusion.3), channel_id=5, replica_groups=mesh['batch_0'=2,'batch_1'=4,'batch_2'=8,'batch_3'=2,'rep'=2] {'batch_3'}, dimensions={0}, use_global_device_ids=true | all-gather | bytes 196608 | tf_op jit(solution)/shard_map/all_gather | solution.py:57
  236.8 0.1 fusion.76
  236.9 0.8 dynamic_slice.11
  237.8 0.8 gather_fusion
  238.6 0.7 subtract_reduce_fusion
  239.3 5.9 %psum.35 = f32[]{:T(128)} all-reduce(f32[]{:T(128)} %get-tuple-element.7), channel_id=1, replica_groups=mesh['batch_0'=2,'batch_1'=4,'batch_2'=8,'batch_3'=2,'rep'=2] {'batch_0'}, use_global_device_ids=true, to_apply=%region_5.6 | all-reduce | flops 1 | bytes 8 | tf_op jit(solution)/shard_map/psum | solution.py:76
  245.2 9.5 %psum.36 = f32[]{:T(128)} all-reduce(f32[]{:T(128)} %psum.35), channel_id=1, replica_groups=mesh['batch_0'=2,'batch_1'=4,'batch_2'=8,'batch_3'=2,'rep'=2] {'batch_1'}, use_global_device_ids=true, to_apply=%region_6.7 | all-reduce | flops 1 | bytes 8 | tf_op jit(solution)/shard_map/psum | solution.py:76
  254.7 13.1 %psum.37 = f32[]{:T(128)} all-reduce(f32[]{:T(128)} %psum.36), channel_id=1, replica_groups=mesh['batch_0'=2,'batch_1'=4,'batch_2'=8,'batch_3'=2,'rep'=2] {'batch_2'}, use_global_device_ids=true, to_apply=%region_7.8 | all-reduce | flops 1 | bytes 8 | tf_op jit(solution)/shard_map/psum | solution.py:76
  267.8 9.0 %psum.38 = f32[]{:T(128)} all-reduce(f32[]{:T(128)} %psum.37), channel_id=1, replica_groups=mesh['batch_0'=2,'batch_1'=4,'batch_2'=8,'batch_3'=2,'rep'=2] {'batch_3'}, use_global_device_ids=true, to_apply=%region_8.9 | all-reduce | flops 1 | bytes 8 | tf_op jit(solution)/shard_map/psum | solution.py:76
  276.9 11.5 %fusion.14 = f32[128,1024]{1,0:T(8,128)} fusion(bf16[8192,1024]{1,0:T(8,128)(2,1)} %all-gather.12.cloned.1.call-done, f32[128,8192]{1,0:T(8,128)} %get-tuple-element.19, s32[8192]{0:T(1024)S(1)} %iota_subtract_fusion, f32[8192]{0:T(1024)S(1)} %log_add_fusion, f32[128]{0:T(128)S(1)} %log_add_fusion.1, s32[128]{0:T(128)S(1)} %iota_subtract_fusion.1, ...), kind=kOutput, calls=%fused_computation.22 | convolution fusion | flops 2157051904 | bytes 21578756 | tf_op jit(solution)/shard_map/dot_general | solution.py:135
  288.4 3.5 all-to-all-start.1
  291.9 15.4 %psum.39 = f32[]{:T(128)} all-reduce(f32[]{:T(128)} %psum.38), channel_id=1, replica_groups=mesh['batch_0'=2,'batch_1'=4,'batch_2'=8,'batch_3'=2,'rep'=2] {'rep'}, use_global_device_ids=true, to_apply=%region_9.10 | all-reduce | flops 1 | bytes 8 | tf_op jit(solution)/shard_map/psum | solution.py:76
  308.0 179.3 %all-gather.8 = f32[128,1,128]{2,1,0:T(1,128)S(1)} all-gather(f32[1,1,128]{2,1,0:T(1,128)S(1)} %fusion.83), channel_id=1, replica_groups=mesh['batch_0'=2,'batch_1'=4,'batch_2'=8,'batch_3'=2,'rep'=2] {'batch_0'..., dimensions={0}, use_global_device_ids=true | all-gather | bytes 66048 | tf_op jit(solution)/shard_map/all_gather | solution.py:138
  487.2 0.7 reduce_sum.39
  488.0 31.9 %fusion.15 = f32[64,1024]{1,0:T(8,128)} fusion(bf16[16384,1024]{1,0:T(8,128)(2,1)} %all-gather.14.cloned.1.call-done, bf16[64,1024]{1,0:T(8,128)(2,1)S(1)} %copy-done, s32[64]{0:T(128)S(1)} %iota_add_fusion, f32[16384]{0:T(1024)S(1)} %bitcast.318, f32[64]{0:T(128)S(1)} %get-tuple-element.8, f32[]{:T(128)} %bitcast.317, f32[]{:T(128)S(6)} %mul.358), kind=kOutput, calls=%fused_computation.23 | convolution fusion | flops 4303421440 | bytes 34013704 | tf_op jit(solution)/shard_map/dot_general | solution.py:152
  (16 shorter events, 0.2 us)
Async XLA Ops:
  7.2 159.9 %all-gather.12.cloned.1.call-start = ((), (), s32[]{:S(2)}) async-start(), calls=%async_computation.2 | async-start | bytes 16908288 | tf_op jit(solution)/shard_map/all_gather | solution.py:106
  7.9 480.1 %all-gather.14.cloned.1.call-start = ((), (), s32[]{:S(2)}) async-start(), calls=%async_computation.3 | async-start | bytes 33816576 | tf_op jit(solution)/shard_map/all_gather | solution.py:140
  184.8 53.7 %all-to-all-start = ((f32[2,2,128]{2,1,0:T(2,128)}), f32[2,2,128]{2,1,0:T(2,128)S(1)}, u32[]{:S(2)}, u32[]{:S(2)}) async-start(f32[2,2,128]{2,1,0:T(2,128)} %broadcast_in_dim.4), calls=%async_computation | async-start | bytes 4096 | tf_op jit(solution)/shard_map/all_to_all | solution.py:14
  276.9 211.1 %copy-start = (bf16[64,1024]{1,0:T(8,128)(2,1)S(1)}, bf16[64,1024]{1,0:T(8,128)(2,1)}, u32[]{:S(2)}) copy-start(bf16[64,1024]{1,0:T(8,128)(2,1)} %param.4) | copy-start | bytes 393220
  288.4 198.9 %all-to-all-start.1 = ((f32[2,64,1024]{2,1,0:T(8,128)}), f32[2,64,1024]{2,1,0:T(8,128)S(1)}, u32[]{:S(2)}, u32[]{:S(2)}) async-start(f32[2,64,1024]{2,1,0:T(8,128)} %bitcast.46), calls=%async_computation.1 | async-start | bytes 1048576 | tf_op jit(solution)/shard_map/all_to_all | solution.py:87
Sparse Core Ops, SparseCore 0:
  11.6 155.4 all-gather.11
  170.7 214.5 all-gather.13
where the time goes:
time: 528 us
  blocking collectives  280 us (53%)
  waiting for transfers between devices  159 us (30%)
  matrix products  56.9 us (11%)
  between operations  16.6 us (3%)
  starting transfers between devices  6.79 us (1%)
  other arithmetic  6.55 us (1%)
    all_gather x1, blocking collectives, body(): all_rows_lse = lax.all_gather(row_lse, BATCH, axis=0, tiled=True)  179 us
    all_gather x1, waiting for transfers between devices, body(): whole_text = lax.all_gather(text_embed, BATCH, axis=0, tiled=True)  158 us
    psum x5, blocking collectives, over_axes(): return functools.reduce(lax.psum, axes, array)  53 us
    all_gather x4, blocking collectives, collected_together(): both, at, found = (lax.all_gather(jnp.concatenate(lines), axis), 0, {})  47.2 us
    dot_general x1, matrix products, body(): jnp.dot(weights_block, fragment, preferred_element_type=jnp.float32)  31.9 us
    dot_general x1, matrix products, body(): lax.dot_general(image_embed, whole_text, (((1,), (1,)), ((), ())), prefer...  13.5 us
    dot_general x1, matrix products, body(): jnp.dot(weights, whole_text, preferred_element_type=jnp.float32)  11.5 us
  transfers between devices with their start and end apart: 4, of which 1 were waited for; matrix products, arithmetic and copies ran while one was open for 6% of the time, Pallas kernels for 0%

commit v1 on v0

--- a/solution.py
+++ b/solution.py
@@ -135,7 +135,9 @@
         scale_value * 0.5 * jnp.dot(weights, whole_text, preferred_element_type=jnp.float32)
     )
     image_grad = sum_at_owner(image_part, "rep", 0)
-    all_rows_lse = lax.all_gather(row_lse, BATCH, axis=0, tiled=True)
+    all_rows_lse = jnp.concatenate(
+        lax.all_to_all(jnp.stack([row_lse] * lax.axis_size(BATCH)), BATCH, 0, 0), axis=0
+    )
     own_first = (2 * batch_index + rep_index) * half_rows
     fragment = lax.all_gather(image_embed, BATCH, axis=0, tiled=True)
     scores_back = scale_value * lax.dot_general(

time: 528 us -> 421 us (0.80)
  blocking collectives: 280 us -> 91.9 us
  waiting for transfers between devices: 159 us -> 229 us
  starting transfers between devices: 6.79 us -> 15.8 us
    all_gather x1 -> x0, blocking collectives: 179 us -> none  [body(): all_rows_lse = lax.all_gather(row_lse, BATCH, axis=0, tiled=True)]
    all_gather x1, waiting for transfers between devices: 0.01 us -> 63.3 us  [body(): fragment = lax.all_gather(image_embed, BATCH, axis=0, tiled=True)]
    all_to_all x0 -> x1, starting transfers between devices: none -> 8.87 us  [body(): lax.all_to_all(jnp.stack([row_lse] * lax.axis_size(BATCH)), BATCH, 0, 0)]
    psum x5, blocking collectives: 53 us -> 44.7 us  [over_axes(): return functools.reduce(lax.psum, axes, array)]
    all_to_all x1, waiting for transfers between devices: 0.01 us -> 6.68 us  [sum_at_owner(): lax.all_to_all(parts, axis, split_axis=0, concat_axis=0, tiled=True)]
  transfers between devices with their start and end apart: 4 -> 5, of which waited for: 1 -> 3; matrix products, arithmetic and copies ran while one was open for 6% -> 8% of each run, Pallas kernels for 0% -> 0%
where the time goes in v1:
time: 421 us; the launch traced here: 420 us
  waiting for transfers between devices  229 us (54%)
  blocking collectives  91.9 us (22%)
  matrix products  57.2 us (14%)
  between operations  16.6 us (4%)
  starting transfers between devices  15.8 us (4%)
  other arithmetic  6.53 us (2%)
    all_gather x1, waiting for transfers between devices, body(): whole_text = lax.all_gather(text_embed, BATCH, axis=0, tiled=True)  158 us
    all_gather x1, waiting for transfers between devices, body(): fragment = lax.all_gather(image_embed, BATCH, axis=0, tiled=True)  63.3 us
    all_gather x4, blocking collectives, collected_together(): both, at, found = (lax.all_gather(jnp.concatenate(lines), axis), 0, {})  47.2 us
    psum x5, blocking collectives, over_axes(): return functools.reduce(lax.psum, axes, array)  44.7 us
    dot_general x1, matrix products, body(): jnp.dot(weights_block, fragment, preferred_element_type=jnp.float32)  31.9 us
    dot_general x1, matrix products, body(): lax.dot_general(image_embed, whole_text, (((1,), (1,)), ((), ())), prefer...  13.5 us
    dot_general x1, matrix products, body(): jnp.dot(weights, whole_text, preferred_element_type=jnp.float32)  11.7 us
    all_to_all x1, starting transfers between devices, body(): lax.all_to_all(jnp.stack([row_lse] * lax.axis_size(BATCH)), BATCH, 0, 0)  8.87 us
  transfers between devices with their start and end apart: 5, of which 3 were waited for; matrix products, arithmetic and copies ran while one was open for 8% of the time, Pallas kernels for 0%

profile of v1, /device:TPU:1, one launch (start us, length us, event | category | flops | bytes accessed | tf_op | source)
XLA Modules:
  0.0 420.2 jit_solution(7607220219119610006)
XLA Ops:
  7.2 0.7 all-gather.11.cloned.1.call-update
  7.9 0.7 all-gather.13.cloned.1.call-update
  9.4 157.8 %all-gather.11.cloned.1.call-done = bf16[8192,1024]{1,0:T(8,128)(2,1)} async-done(((bf16[64,1024]{1,0:T(8,128)(2,1)}), bf16[8192,1024]{1,0:T(8,128)(2,1)}) %all-gather.11.cloned.1.call-update) | async-done | bytes 16777232 | tf_op jit(solution)/shard_map/all_gather | solution.py:106
  167.1 13.5 %fusion.72 = (f32[128]{0:T(128)S(1)}, f32[8192]{0:T(1024)S(1)}, f32[128,8192]{1,0:T(8,128)}) fusion(bf16[128,1024]{1,0:T(8,128)(2,1)} %param.3, bf16[8192,1024]{1,0:T(8,128)(2,1)} %all-gather.11.cloned.1.call-done, f32[]{:T(128)} %bitcast.305), kind=kOutput, calls=%fused_computation.126 | convolution fusion | flops 2150621184 | bytes 21266948 | tf_op jit(solution)/shard_map/dot_general | solution.py:107
  180.7 3.6 exponential_reduce_fusion.1
  184.2 0.6 broadcast_in_dim.4
  184.8 3.2 all-to-all-start
  188.1 5.3 %all-gather.4 = f32[2,2,8192]{2,1,0:T(2,128)S(1)} all-gather(f32[1,2,8192]{2,1,0:T(2,128)S(1)} %maximum_bitcast_fusion), channel_id=2, replica_groups=mesh['batch_0'=2,'batch_1'=4,'batch_2'=8,'batch_3'=2,'rep'=2] {'batch_0'}, dimensions={0}, use_global_device_ids=true | all-gather | bytes 196608 | tf_op jit(solution)/shard_map/all_gather | solution.py:57
  193.4 0.1 fusion.47
  193.6 11.0 %all-gather.5 = f32[4,2,8192]{2,1,0:T(2,128)S(1)} all-gather(f32[1,2,8192]{2,1,0:T(2,128)S(1)} %maximum_bitcast_fusion.1), channel_id=3, replica_groups=mesh['batch_0'=2,'batch_1'=4,'batch_2'=8,'batch_3'=2,'rep'=2] {'batch_1'}, dimensions={0}, use_global_device_ids=true | all-gather | bytes 327680 | tf_op jit(solution)/shard_map/all_gather | solution.py:57
  204.6 0.3 fusion.38
  205.0 21.2 %all-gather.6 = f32[8,2,8192]{2,1,0:T(2,128)S(1)} all-gather(f32[1,2,8192]{2,1,0:T(2,128)S(1)} %maximum_bitcast_fusion.2), channel_id=4, replica_groups=mesh['batch_0'=2,'batch_1'=4,'batch_2'=8,'batch_3'=2,'rep'=2] {'batch_2'}, dimensions={0}, use_global_device_ids=true | all-gather | bytes 589824 | tf_op jit(solution)/shard_map/all_gather | solution.py:57
  226.2 0.7 fusion.17
  226.9 0.1 maximum_bitcast_fusion.3
  227.0 9.8 %all-gather.7 = f32[2,2,8192]{2,1,0:T(2,128)S(1)} all-gather(f32[1,2,8192]{2,1,0:T(2,128)S(1)} %maximum_bitcast_fusion.3), channel_id=5, replica_groups=mesh['batch_0'=2,'batch_1'=4,'batch_2'=8,'batch_3'=2,'rep'=2] {'batch_3'}, dimensions={0}, use_global_device_ids=true | all-gather | bytes 196608 | tf_op jit(solution)/shard_map/all_gather | solution.py:57
  236.8 0.1 fusion.76
  236.9 11.7 %fusion.14 = f32[128,1024]{1,0:T(8,128)} fusion(bf16[8192,1024]{1,0:T(8,128)(2,1)} %all-gather.11.cloned.1.call-done, f32[128,8192]{1,0:T(8,128)} %get-tuple-element.19, s32[8192]{0:T(1024)S(1)} %iota_subtract_fusion, f32[8192]{0:T(1024)S(1)} %log_add_fusion, f32[128]{0:T(128)S(1)} %log_add_fusion.1, s32[128]{0:T(128)S(1)} %iota_subtract_fusion.1, ...), kind=kOutput, calls=%fused_computation.22 | convolution fusion | flops 2157051904 | bytes 21578756 | tf_op jit(solution)/shard_map/dot_general | solution.py:135
  248.7 3.7 all-to-all-start.1
  252.4 0.8 dynamic_slice.11
  253.2 0.8 gather_fusion
  254.0 6.7 %all-to-all-done.1 = f32[2,64,1024]{2,1,0:T(8,128)S(1)} async-done(((f32[2,64,1024]{2,1,0:T(8,128)}), f32[2,64,1024]{2,1,0:T(8,128)S(1)}, u32[]{:S(2)}, u32[]{:S(2)}) %all-to-all-start.1) | async-done | bytes 524320 | tf_op jit(solution)/shard_map/all_to_all | solution.py:87
  260.7 0.7 stack.2
  261.4 8.9 %all-to-all-start.2 = ((f32[128,1,128]{2,1,0:T(1,128)}), f32[128,1,128]{2,1,0:T(1,128)S(1)}, u32[]{:S(2)}, u32[]{:S(2)}) async-start(f32[128,1,128]{2,1,0:T(1,128)} %stack.2), calls=%async_computation.2 | async-start | bytes 131072 | tf_op jit(solution)/shard_map/all_to_all | solution.py:139
  270.2 0.7 subtract_reduce_fusion
  270.9 6.8 %psum.35 = f32[]{:T(128)} all-reduce(f32[]{:T(128)} %get-tuple-element.7), channel_id=1, replica_groups=mesh['batch_0'=2,'batch_1'=4,'batch_2'=8,'batch_3'=2,'rep'=2] {'batch_0'}, use_global_device_ids=true, to_apply=%region_5.6 | all-reduce | flops 1 | bytes 8 | tf_op jit(solution)/shard_map/psum | solution.py:76
  277.7 10.5 %psum.36 = f32[]{:T(128)} all-reduce(f32[]{:T(128)} %psum.35), channel_id=1, replica_groups=mesh['batch_0'=2,'batch_1'=4,'batch_2'=8,'batch_3'=2,'rep'=2] {'batch_1'}, use_global_device_ids=true, to_apply=%region_6.7 | all-reduce | flops 1 | bytes 8 | tf_op jit(solution)/shard_map/psum | solution.py:76
  288.2 15.4 %psum.37 = f32[]{:T(128)} all-reduce(f32[]{:T(128)} %psum.36), channel_id=1, replica_groups=mesh['batch_0'=2,'batch_1'=4,'batch_2'=8,'batch_3'=2,'rep'=2] {'batch_2'}, use_global_device_ids=true, to_apply=%region_7.8 | all-reduce | flops 1 | bytes 8 | tf_op jit(solution)/shard_map/psum | solution.py:76
  303.6 7.0 %psum.38 = f32[]{:T(128)} all-reduce(f32[]{:T(128)} %psum.37), channel_id=1, replica_groups=mesh['batch_0'=2,'batch_1'=4,'batch_2'=8,'batch_3'=2,'rep'=2] {'batch_3'}, use_global_device_ids=true, to_apply=%region_8.9 | all-reduce | flops 1 | bytes 8 | tf_op jit(solution)/shard_map/psum | solution.py:76
  310.6 5.0 %psum.39 = f32[]{:T(128)} all-reduce(f32[]{:T(128)} %psum.38), channel_id=1, replica_groups=mesh['batch_0'=2,'batch_1'=4,'batch_2'=8,'batch_3'=2,'rep'=2] {'rep'}, use_global_device_ids=true, to_apply=%region_9.10 | all-reduce | flops 1 | bytes 8 | tf_op jit(solution)/shard_map/psum | solution.py:76
  316.3 0.7 reduce_sum.39
  317.0 63.3 %all-gather.13.cloned.1.call-done = bf16[16384,1024]{1,0:T(8,128)(2,1)} async-done(((bf16[128,1024]{1,0:T(8,128)(2,1)}), bf16[16384,1024]{1,0:T(8,128)(2,1)}) %all-gather.13.cloned.1.call-update) | async-done | bytes 33554448 | tf_op jit(solution)/shard_map/all_gather | solution.py:142
  380.4 31.9 %fusion.15 = f32[64,1024]{1,0:T(8,128)} fusion(bf16[16384,1024]{1,0:T(8,128)(2,1)} %all-gather.13.cloned.1.call-done, bf16[64,1024]{1,0:T(8,128)(2,1)S(1)} %copy-done, s32[64]{0:T(128)S(1)} %iota_add_fusion, f32[16384]{0:T(1024)S(1)} %bitcast.308, f32[64]{0:T(128)S(1)} %get-tuple-element.8, f32[]{:T(128)} %bitcast.307, f32[]{:T(128)S(6)} %mul.362), kind=kOutput, calls=%fused_computation.23 | convolution fusion | flops 4303421440 | bytes 34013704 | tf_op jit(solution)/shard_map/dot_general | solution.py:154
  (17 shorter events, 0.4 us)
Async XLA Ops:
  7.2 159.9 %all-gather.11.cloned.1.call-start = ((), (), s32[]{:S(2)}) async-start(), calls=%async_computation.3 | async-start | bytes 16908288 | tf_op jit(solution)/shard_map/all_gather | solution.py:106
  7.9 372.5 %all-gather.13.cloned.1.call-start = ((), (), s32[]{:S(2)}) async-start(), calls=%async_computation.4 | async-start | bytes 33816576 | tf_op jit(solution)/shard_map/all_gather | solution.py:142
  184.8 52.1 %all-to-all-start = ((f32[2,2,128]{2,1,0:T(2,128)}), f32[2,2,128]{2,1,0:T(2,128)S(1)}, u32[]{:S(2)}, u32[]{:S(2)}) async-start(f32[2,2,128]{2,1,0:T(2,128)} %broadcast_in_dim.4), calls=%async_computation | async-start | bytes 4096 | tf_op jit(solution)/shard_map/all_to_all | solution.py:14
  236.9 143.4 %copy-start = (bf16[64,1024]{1,0:T(8,128)(2,1)S(1)}, bf16[64,1024]{1,0:T(8,128)(2,1)}, u32[]{:S(2)}) copy-start(bf16[64,1024]{1,0:T(8,128)(2,1)} %param.4) | copy-start | bytes 393220
  248.7 12.0 %all-to-all-start.1 = ((f32[2,64,1024]{2,1,0:T(8,128)}), f32[2,64,1024]{2,1,0:T(8,128)S(1)}, u32[]{:S(2)}, u32[]{:S(2)}) async-start(f32[2,64,1024]{2,1,0:T(8,128)} %bitcast.46), calls=%async_computation.1 | async-start | bytes 1048576 | tf_op jit(solution)/shard_map/all_to_all | solution.py:87
  261.4 55.6 %all-to-all-start.2 = ((f32[128,1,128]{2,1,0:T(1,128)}), f32[128,1,128]{2,1,0:T(1,128)S(1)}, u32[]{:S(2)}, u32[]{:S(2)}) async-start(f32[128,1,128]{2,1,0:T(1,128)} %stack.2), calls=%async_computation.2 | async-start | bytes 131072 | tf_op jit(solution)/shard_map/all_to_all | solution.py:139
Sparse Core Ops, SparseCore 0:
  11.6 155.4 all-gather.10
  170.7 209.5 all-gather.12
